TPU v7x, 256 devices: a whole 4x4x8 slice. The times are simulated.
256 devices in a mesh: dp: 8 (over z_lo, core), fsdp: 32 (over y, x, z_hi).
Axes of the slice: x: 4, y: 4, z: 8 (z_hi: 2, z_lo: 4; z = z_hi * 4 + z_lo), core: 2. Of those that a mesh axis runs over, the one named last changes fastest.
Arguments:
- hidden_states: bfloat16 [1024, 4096], P(('dp', 'fsdp')), may hold values from -400 to 400
- token_ids: int32 [1024], P(('dp', 'fsdp')), may hold values from 0 to 4095
- norm_gain: float32 [4096], replicated, may hold values from 0.5 to 1.5
- ref_gate_w: bfloat16 [4096, 14784], P('dp', 'fsdp'), may hold values from -0.1875 to 0.1875
- ref_up_w: bfloat16 [4096, 14784], P('dp', 'fsdp'), may hold values from -0.1875 to 0.1875
- ref_down_w: bfloat16 [14784, 4096], P('fsdp', 'dp'), may hold values from -0.09375 to 0.09375
- pol_gate_w: bfloat16 [4096, 14784], P('dp', 'fsdp'), may hold values from -0.1875 to 0.1875
- pol_up_w: bfloat16 [4096, 14784], P('dp', 'fsdp'), may hold values from -0.1875 to 0.1875
- pol_down_w: bfloat16 [14784, 4096], P('fsdp', 'dp'), may hold values from -0.09375 to 0.09375
- sample_lengths: int32 [8, 32], P('dp'), may hold values from 1 to 24, 128 in all within a row
- prompt_index: int32 [8, 32], P('dp'), may hold values from 0 to 3, as said below
- rewards: float32 [8, 32], P('dp'), may hold values from -6 to 6
Outputs:
- grad_gate: float32 [4096, 14784], P('dp', 'fsdp')
- grad_up: float32 [4096, 14784], P('dp', 'fsdp')
- grad_down: float32 [14784, 4096], P('fsdp', 'dp')
- advantage: float32 [8, 32], P('dp')
Inputs may be any that keep to these rules, and one draw needn't show every extreme that they name: `prompt_index`: in each row, every prompt from 0 to 3 is answered by exactly 8 samples. `sample_lengths`: each row sums to 128.
All inputs are finite; a program needn't handle non-finite values.
Results may differ from a plain program's by a relative error of at most 0.013.
Values may be sent and summed in bfloat16 or wider, within the bound.
A program may use at most 64 MiB of HBM per device.

v0:
```python
import jax
import jax.numpy as jnp
from jax import lax
from jax.sharding import PartitionSpec as P

K = 8
EPSILON = 1e-06
KL_WEIGHT = 0.05


def cut_along(shard, dim, count):
    lengths = shard.shape
    tiles = shard.reshape(*lengths[:dim], count, lengths[dim] // count, *lengths[dim + 1 :])
    return jnp.moveaxis(tiles, dim, 0)


def sent_and_summed(shard, axis, dim):
    tiles = cut_along(shard, dim, lax.axis_size(axis))
    arrived = lax.all_to_all(tiles, axis, split_axis=0, concat_axis=0, tiled=True)
    return arrived.sum(axis=0)


def copy_for_each(shard, axis):
    copies = jnp.broadcast_to(shard, (lax.axis_size(axis), *shard.shape))
    return lax.all_to_all(copies, axis, split_axis=0, concat_axis=0, tiled=True)


def laid_out(tiles, dim):
    lengths = list(tiles.shape[1:])
    lengths[dim] *= tiles.shape[0]
    return jnp.moveaxis(tiles, 0, dim).reshape(lengths)


def gather_directly(shard, axis, dim):
    tiles = copy_for_each(shard, axis)
    return laid_out(tiles, dim)


def all_in_one(shard, axis):
    leaves = jax.tree.leaves(shard)
    sequence = sorted(range(len(leaves)), key=lambda k: -leaves[k].size)
    width = (1, *leaves[sequence[0]].shape)[-1]
    lines = [
        jnp.pad(leaves[k].reshape(-1), (0, -leaves[k].size % width)).reshape(-1, width)
        for k in sequence
    ]
    both, at, found = (copy_for_each(jnp.concatenate(lines), axis), 0, {})
    for k, line in zip(sequence, lines):
        slab = both[:, at : at + len(line)].reshape(len(both), -1)
        found[k] = slab[:, : leaves[k].size].reshape(-1, *leaves[k].shape)
        at += len(line)
    numbers = iter(range(len(leaves)))
    return jax.tree.map(lambda _: found[next(numbers)], shard)


def joined_by_halves(pieces, combine):
    while len(jax.tree.leaves(pieces)[0]) > 1:
        pieces = jax.vmap(combine)(
            *(jax.tree.map(lambda part: part[side::2], pieces) for side in (0, 1))
        )
    return jax.tree.map(lambda part: part[0], pieces)


def joined_all(shard, axis, combine):
    pieces = all_in_one(shard, axis)
    return joined_by_halves(pieces, combine)


def taken_together(shard, axis):
    return copy_for_each(shard, axis).sum(axis=0)


def normalize(states, norm_gain):
    values = states.astype(jnp.float32)
    factor = lax.rsqrt(jnp.mean(values * values, axis=-1, keepdims=True) + EPSILON)
    return (values * factor * norm_gain).astype(jnp.bfloat16)


def combine_totals(first, second):
    row_peak = jnp.maximum(first[0], second[0])
    summed = first[1] * jnp.exp(first[0] - row_peak) + second[1] * jnp.exp(second[0] - row_peak)
    return (row_peak, summed, first[2] + second[2])


def grouped_product(left_rows, right_rows, groups, members):
    group_depth = left_rows.shape[0] // (groups * members)
    left_four = left_rows.reshape(members, groups, group_depth, left_rows.shape[1])
    right_four = right_rows.reshape(members, groups, group_depth, right_rows.shape[1])
    terms = jnp.einsum("jgta,jgtb->gab", left_four, right_four, preferred_element_type=jnp.float32)
    rounded = lax.optimization_barrier(terms.astype(jnp.bfloat16))
    return jnp.sum(rounded.astype(jnp.float32), axis=0)


def column_section(normed_cols, state_cols, ids_all, weight_sets, group_index):
    col_width = state_cols.shape[1]
    unit_count = weight_sets[0][0].shape[1]
    in_weights = jnp.concatenate(
        [matrix for triple in weight_sets for matrix in triple[:2]], axis=1
    )
    pre_sums = sent_and_summed(
        jnp.dot(normed_cols, in_weights, preferred_element_type=jnp.float32), "dp", 0
    )
    activations = []
    for model_index in range(len(weight_sets)):
        gate_pre = pre_sums[:, 2 * model_index * unit_count : (2 * model_index + 1) * unit_count]
        up_pre = pre_sums[
            :, (2 * model_index + 1) * unit_count : (2 * model_index + 2) * unit_count
        ]
        activations.append(jax.nn.silu(gate_pre) * up_pre)
    hidden_local = jnp.concatenate(activations, axis=1).astype(jnp.bfloat16)
    hidden_all = gather_directly(hidden_local, "dp", 0)

    def project_out():
        pieces = [
            jnp.dot(
                hidden_all[:, model_index * unit_count : (model_index + 1) * unit_count],
                weight_sets[model_index][2],
                preferred_element_type=jnp.float32,
            )
            for model_index in range(len(weight_sets))
        ]
        return jnp.concatenate(pieces, axis=1)

    out_cols = sent_and_summed(project_out(), "fsdp", 0)
    states = state_cols.astype(jnp.float32)
    col_ids = jnp.arange(col_width, dtype=jnp.int32) + group_index * col_width
    logits_list = []
    peaks = []
    sums = []
    picks = []
    for model_index in range(len(weight_sets)):
        logits = states + out_cols[:, model_index * col_width : (model_index + 1) * col_width]
        row_peak = jnp.max(logits, axis=1)
        logits_list.append(logits)
        peaks.append(row_peak)
        sums.append(jnp.sum(jnp.exp(logits - row_peak[:, None]), axis=1))
        picks.append(jnp.sum(jnp.where(col_ids[None, :] == ids_all[:, None], logits, 0.0), axis=1))
    row_peak, summed, picked = joined_all(
        (jnp.stack(peaks, axis=1), jnp.stack(sums, axis=1), jnp.stack(picks, axis=1)),
        "dp",
        combine_totals,
    )
    log_total = row_peak + jnp.log(summed)
    return (pre_sums, hidden_all, logits_list, log_total, picked - log_total)


def leave_one_out(log_gap, inside, prompt_index, rewards):
    divergence = taken_together(jnp.sum(log_gap[:, None] * inside, axis=0), "fsdp")
    scores = rewards[0] - KL_WEIGHT * divergence
    same_prompt = (prompt_index[0][:, None] == prompt_index[0][None, :]).astype(jnp.float32)
    others = jnp.sum(same_prompt * scores[None, :], axis=1) - scores
    advantage = scores - others / (K - 1)
    weight = jnp.sum(inside * advantage[None, :], axis=1)
    return (advantage, weight)


def local(
    hidden_states,
    token_ids,
    norm_gain,
    ref_gate_w,
    ref_up_w,
    ref_down_w,
    pol_gate_w,
    pol_up_w,
    pol_down_w,
    sample_lengths,
    prompt_index,
    rewards,
):
    token_count = hidden_states.shape[0]
    groups = lax.axis_size("dp")
    members = lax.axis_size("fsdp")
    group_index = lax.axis_index("dp")
    member_index = lax.axis_index("fsdp")
    unit_count = pol_gate_w.shape[1]
    normed = normalize(hidden_states, norm_gain)
    normed_mixed, state_cols = (
        lax.all_to_all(normed, "dp", split_axis=1, concat_axis=0, tiled=True),
        lax.all_to_all(hidden_states, "dp", split_axis=1, concat_axis=0, tiled=True),
    )
    normed_cols = lax.all_gather(normed_mixed, "fsdp", axis=0, tiled=True)
    ids_all = gather_directly(token_ids, "dp", 0)
    own_start = group_index * token_count
    position = member_index * token_count + jnp.arange(token_count, dtype=jnp.int32)
    sample_ends = jnp.cumsum(sample_lengths[0])
    sample_starts = sample_ends - sample_lengths[0]
    inside = (
        (position[:, None] >= sample_starts[None, :]) & (position[:, None] < sample_ends[None, :])
    ).astype(jnp.float32)
    pre_sums, hidden_all, logits_list, log_total, logprob = column_section(
        normed_cols,
        state_cols,
        ids_all,
        [(ref_gate_w, ref_up_w, ref_down_w), (pol_gate_w, pol_up_w, pol_down_w)],
        group_index,
    )
    ref_own = lax.dynamic_slice_in_dim(logprob[:, 0], own_start, token_count, 0)
    pol_own = lax.dynamic_slice_in_dim(logprob[:, 1], own_start, token_count, 0)
    advantage, weight = leave_one_out(pol_own - ref_own, inside, prompt_index, rewards)
    weight_all = gather_directly(weight, "dp", 0)
    col_width = state_cols.shape[1]
    col_ids = jnp.arange(col_width, dtype=jnp.int32) + group_index * col_width
    onehot_cols = (col_ids[None, :] == ids_all[:, None]).astype(jnp.float32)
    grad_cols = (
        -weight_all[:, None] * (onehot_cols - jnp.exp(logits_list[1] - log_total[:, 1:2]))
    ).astype(jnp.bfloat16)
    grad_cols_all = lax.all_gather(grad_cols, "fsdp", axis=0, tiled=True)
    pol_hidden = hidden_all[:, unit_count : 2 * unit_count]
    grad_down = grouped_product(pol_hidden, grad_cols_all, groups, members)
    grad_hidden = sent_and_summed(
        lax.dot_general(
            grad_cols_all, pol_down_w, (((1,), (1,)), ((), ())), preferred_element_type=jnp.float32
        ),
        "dp",
        0,
    )
    gate_pre = pre_sums[:, 2 * unit_count : 3 * unit_count]
    up_pre = pre_sums[:, 3 * unit_count : 4 * unit_count]
    sigmoid_gate = jax.nn.sigmoid(gate_pre)
    grad_gate_pre = grad_hidden * up_pre * sigmoid_gate * (1.0 + gate_pre * (1.0 - sigmoid_gate))
    grad_up_pre = grad_hidden * gate_pre * sigmoid_gate
    gate_grads = jnp.concatenate(
        [grad_gate_pre.astype(jnp.bfloat16), grad_up_pre.astype(jnp.bfloat16)], axis=1
    )
    gate_grads_all = gather_directly(gate_grads, "dp", 0)
    grad_inner = grouped_product(normed_cols, gate_grads_all, groups, members)
    return (grad_inner[:, :unit_count], grad_inner[:, unit_count:], grad_down, advantage[None, :])


def solution(mesh):
    return jax.shard_map(
        local,
        mesh=mesh,
        in_specs=(
            P(("dp", "fsdp"), None),
            P(("dp", "fsdp")),
            P(),
            P("dp", "fsdp"),
            P("dp", "fsdp"),
            P("fsdp", "dp"),
            P("dp", "fsdp"),
            P("dp", "fsdp"),
            P("fsdp", "dp"),
            P("dp", None),
            P("dp", None),
            P("dp", None),
        ),
        out_specs=(P("dp", "fsdp"), P("dp", "fsdp"), P("fsdp", "dp"), P("dp", None)),
        check_vma=False,
    )
```

profile of v0, /device:TPU:1, one launch (start us, length us, event | category | flops | bytes accessed | tf_op | source)
XLA Modules:
  0.0 705.4 jit_solution(487625159166085097)
XLA Ops:
  9.0 12.2 %all_to_all.80 = bf16[4,8,512]{2,0,1:T(4,128)(2,1)S(1)} all-to-all(bf16[4,8,512]{2,0,1:T(4,128)(2,1)S(1)} %bitcast.86), channel_id=1, replica_groups=mesh['dp'=8,'fsdp'=32] {'dp'}, dimensions={1} | all-to-all | bytes 65536 | tf_op jit(solution)/shard_map/all_to_all | solution.py:179
  21.9 8.4 %concatenate.16 = bf16[512,1848]{0,1:T(8,128)(2,1)S(1)} concatenate(bf16[512,462]{0,1:T(8,128)(2,1)} %param.15, bf16[512,462]{0,1:T(8,128)(2,1)} %param.16, bf16[512,462]{0,1:T(8,128)(2,1)} %param.18, bf16[512,462]{0,1:T(8,128)(2,1)} %param.19), dimensions={1} | concatenate | bytes 3784704 | tf_op jit(solution)/shard_map/concatenate | solution.py:97
  30.3 72.1 %all-gather.3.cloned.1.call-done = bf16[1024,512]{1,0:T(8,128)(2,1)} async-done(((bf16[32,512]{1,0:T(8,128)(2,1)}), bf16[1024,512]{1,0:T(8,128)(2,1)}) %all-gather.3.cloned.1.call-update) | async-done | bytes 1048592 | tf_op jit(solution)/shard_map/all_gather | solution.py:182
  102.4 3.4 convolution_bitcast_fusion
  106.3 171.0 %all_to_all.81 = f32[8,128,1848]{1,2,0:T(8,128)} all-to-all(f32[8,128,1848]{1,2,0:T(8,128)S(1)} %bitcast.77), channel_id=1, replica_groups=mesh['dp'=8,'fsdp'=32] {'dp'}, dimensions={0} | all-to-all | bytes 15138816 | tf_op jit(solution)/shard_map/all_to_all | solution.py:19
  277.3 3.6 reduce_sum.129
  281.4 47.5 %all_to_all.82 = bf16[8,128,924]{1,2,0:T(8,128)(2,1)S(1)} all-to-all(bf16[8,128,924]{1,2,0:T(8,128)(2,1)S(1)} %broadcast_in_dim.17), channel_id=1, replica_groups=mesh['dp'=8,'fsdp'=32] {'dp'}, dimensions={0} | all-to-all | bytes 3784704 | tf_op jit(solution)/shard_map/all_to_all | solution.py:25
  329.5 4.0 all-to-all-start.5
  334.9 2.1 fusion.27
  338.3 4.6 all-to-all-start.1
  342.9 4.1 pad_maximum_fusion
  347.0 5.3 copy.74
  352.4 5.0 all-to-all-start.4
  359.0 102.3 %all-to-all-done.4 = f32[32,32,1024]{2,1,0:T(8,128)} async-done(((f32[32,32,1024]{2,1,0:T(8,128)}), f32[32,32,1024]{2,1,0:T(8,128)}, u32[]{:S(2)}, u32[]{:S(2)}) %all-to-all-start.4) | async-done | bytes 4194336 | tf_op jit(solution)/shard_map/all_to_all | solution.py:19
  461.2 2.4 reduce_sum.130
  464.9 4.9 all-to-all-start.6
  469.9 4.9 all-to-all-done.6
  475.1 21.5 %all_to_all.83 = f32[32,1,32]{2,1,0:T(1,128)S(1)} all-to-all(f32[32,1,32]{2,1,0:T(1,128)S(1)} %broadcast_in_dim.21), channel_id=1, replica_groups=mesh['dp'=8,'fsdp'=32] {'fsdp'}, dimensions={0} | all-to-all | bytes 8192 | tf_op jit(solution)/shard_map/all_to_all | solution.py:25
  497.6 5.3 all-to-all-start.8
  502.9 4.8 all-to-all-done.8
  508.6 74.4 %all-gather.5.cloned.1.call-done = bf16[1024,512]{1,0:T(8,128)(2,1)} async-done(((bf16[32,512]{1,0:T(8,128)(2,1)}), bf16[1024,512]{1,0:T(8,128)(2,1)}) %all-gather.5.cloned.1.call-update) | async-done | bytes 1048592 | tf_op jit(solution)/shard_map/all_gather | solution.py:208
  583.0 1.9 fusion.34
  585.9 49.0 %all_to_all.84 = f32[8,128,462]{1,2,0:T(8,128)S(1)} all-to-all(f32[8,128,462]{1,2,0:T(8,128)S(1)} %copy.76), channel_id=1, replica_groups=mesh['dp'=8,'fsdp'=32] {'dp'}, dimensions={0} | all-to-all | bytes 3784704 | tf_op jit(solution)/shard_map/all_to_all | solution.py:19
  635.2 1.5 broadcast_in_dim.44
  636.7 5.2 all-to-all-start.10
  646.6 3.6 bitcast_convert_fusion.1
  650.2 1.5 convert_reduce_fusion.1
  651.7 34.2 %all-to-all-done.10 = bf16[8,128,924]{1,2,0:T(8,128)(2,1)} async-done(((bf16[8,128,924]{1,2,0:T(8,128)(2,1)}), bf16[8,128,924]{1,2,0:T(8,128)(2,1)}, u32[]{:S(2)}, u32[]{:S(2)}) %all-to-all-start.10) | async-done | bytes 1892384 | tf_op jit(solution)/shard_map/all_to_all | solution.py:25
  685.9 2.8 copy.78
  688.7 2.2 reshape_reshape.3
  690.9 5.0 bitcast_convert_fusion
  697.1 1.5 fusion.31
  (92 shorter events, 18.7 us)
Async XLA Ops:
  7.2 327.7 %copy-start = (bf16[462,512]{1,0:T(8,128)(2,1)S(1)}, bf16[462,512]{1,0:T(8,128)(2,1)}, u32[]{:S(2)}) copy-start(bf16[462,512]{1,0:T(8,128)(2,1)} %param.20) | copy-start | bytes 1419268
  7.2 95.2 %all-gather.3.cloned.1.call-start = ((), (), s32[]{:S(2)}) async-start(), calls=%async_computation.11 | async-start | bytes 1081344 | tf_op jit(solution)/shard_map/all_gather | solution.py:182
  281.4 47.5 %copy-start.9 = (s32[4]{0:T(128)S(1)}, s32[4]{0:T(128)}, u32[]{:S(2)}) copy-start(s32[4]{0:T(128)} %param.13) | copy-start | bytes 52
  329.5 8.8 %all-to-all-start.5 = ((s32[8,1,4]{2,1,0:T(1,128)}), s32[8,1,4]{2,1,0:T(1,128)S(1)}, u32[]{:S(2)}, u32[]{:S(2)}) async-start(s32[8,1,4]{2,1,0:T(1,128)} %broadcast_in_dim.18), calls=%async_computation.5 | async-start | bytes 8192 | tf_op jit(solution)/shard_map/all_to_all | solution.py:25
  334.9 2.1 copy-start.2
  334.9 2.1 copy-start.7
  338.3 14.0 %all-to-all-start.1 = ((bf16[4,8,512]{2,0,1:T(4,128)(2,1)}), bf16[4,8,512]{2,0,1:T(4,128)(2,1)S(1)}, u32[]{:S(2)}, u32[]{:S(2)}) async-start(bf16[4,8,512]{2,0,1:T(4,128)(2,1)} %bitcast.4), calls=%async_computation.1 | async-start | bytes 65536 | tf_op jit(solution)/shard_map/all_to_all | solution.py:180
  352.4 5.0 copy-start.10
  352.4 108.9 %all-to-all-start.4 = ((f32[32,32,1024]{2,1,0:T(8,128)}), f32[32,32,1024]{2,1,0:T(8,128)}, u32[]{:S(2)}, u32[]{:S(2)}) async-start(f32[32,32,1024]{2,1,0:T(8,128)} %bitcast.78), calls=%async_computation.4 | async-start | bytes 8388608 | tf_op jit(solution)/shard_map/all_to_all | solution.py:19
  359.0 137.7 %copy-start.11 = (f32[1,32]{1,0:T(1,128)S(1)}, f32[1,32]{1,0:T(1,128)}, u32[]{:S(2)}) copy-start(f32[1,32]{1,0:T(1,128)} %param.23) | copy-start | bytes 388
  359.0 137.7 %copy-start.8 = (s32[1,32]{1,0:T(1,128)S(1)}, s32[1,32]{1,0:T(1,128)}, u32[]{:S(2)}) copy-start(s32[1,32]{1,0:T(1,128)} %param.22) | copy-start | bytes 388
  464.9 9.8 %all-to-all-start.6 = ((f32[8,96,2]{1,2,0:T(2,128)}), f32[8,96,2]{1,2,0:T(2,128)S(1)}, u32[]{:S(2)}, u32[]{:S(2)}) async-start(f32[8,96,2]{1,2,0:T(2,128)} %broadcast_in_dim.20), calls=%async_computation.6 | async-start | bytes 16384 | tf_op jit(solution)/shard_map/all_to_all | solution.py:25
  496.9 88.5 %copy-start.12 = (f32[1,32]{1,0:T(1,128)}, f32[1,32]{1,0:T(1,128)S(1)}, u32[]{:S(2)}) copy-start(f32[1,32]{1,0:T(1,128)S(1)} %fusion.24) | copy-start | bytes 388
  497.6 10.2 %all-to-all-start.8 = ((f32[8,1,4]{2,1,0:T(1,128)}), f32[8,1,4]{2,1,0:T(1,128)S(1)}, u32[]{:S(2)}, u32[]{:S(2)}) async-start(f32[8,1,4]{2,1,0:T(1,128)} %broadcast_in_dim.22), calls=%async_computation.8 | async-start | bytes 8192 | tf_op jit(solution)/shard_map/all_to_all | solution.py:25
  502.9 80.1 %all-gather.5.cloned.1.call-start = ((), (), s32[]{:S(2)}) async-start(), calls=%async_computation.12 | async-start | bytes 1081344 | tf_op jit(solution)/shard_map/all_gather | solution.py:208
  636.7 5.2 copy-start.5
  636.7 6.3 copy-start.3
  636.7 49.2 %all-to-all-start.10 = ((bf16[8,128,924]{1,2,0:T(8,128)(2,1)}), bf16[8,128,924]{1,2,0:T(8,128)(2,1)}, u32[]{:S(2)}, u32[]{:S(2)}) async-start(bf16[8,128,924]{1,2,0:T(8,128)(2,1)} %broadcast_in_dim.44), calls=%async_computation.10 | async-start | bytes 3801088 | tf_op jit(solution)/shard_map/all_to_all | solution.py:25
  643.2 1.7 copy-start.4
  645.0 1.6 copy-start.6
  696.0 2.6 copy-start.1
Sparse Core Ops, SparseCore 0:
  22.0 80.3 all-gather.2
  508.7 74.2 all-gather.4
where the time goes:
time: 707 us; the launch traced here: 705 us
  blocking collectives  301 us (43%)
  waiting for transfers between devices  293 us (41%)
  local copies, waits for them, and re-layouts  32.9 us (5%)
  starting transfers between devices  29.1 us (4%)
  other arithmetic  17.8 us (3%)
  matrix products  16.8 us (2%)
  between operations  14.4 us (2%)
    all_to_all x2, blocking collectives, sent_and_summed(): lax.all_to_all(tiles, axis, split_axis=0, concat_axis=0, tiled=True)  220 us
    all_to_all x1, waiting for transfers between devices, sent_and_summed(): lax.all_to_all(tiles, axis, split_axis=0, concat_axis=0, tiled=True)  102 us
    all_gather x1, waiting for transfers between devices, local(): grad_cols_all = lax.all_gather(grad_cols, 'fsdp', axis=0, tiled=True)  74.4 us
    all_gather x1, waiting for transfers between devices, local(): normed_cols = lax.all_gather(normed_mixed, 'fsdp', axis=0, tiled=True)  72.1 us
    all_to_all x2, blocking collectives, copy_for_each(): return lax.all_to_all(copies, axis, split_axis=0, concat_axis=0, tiled=True)  69 us
    all_to_all x4, waiting for transfers between devices, copy_for_each(): return lax.all_to_all(copies, axis, split_axis=0, concat_axis=0, tiled=True)  44.5 us
    all_to_all x4, starting transfers between devices, copy_for_each(): return lax.all_to_all(copies, axis, split_axis=0, concat_axis=0, tiled=True)  19.4 us
  transfers between devices with their start and end apart: 8, of which 7 were waited for; matrix products, arithmetic and copies ran while one was open for 5% of the time, Pallas kernels for 0%

commit v1 on v0

--- a/solution.py
+++ b/solution.py
@@ -205,7 +205,9 @@
     grad_cols = (
         -weight_all[:, None] * (onehot_cols - jnp.exp(logits_list[1] - log_total[:, 1:2]))
     ).astype(jnp.bfloat16)
-    grad_cols_all = lax.all_gather(grad_cols, "fsdp", axis=0, tiled=True)
+    grad_cols_all = jnp.concatenate(
+        lax.all_to_all(jnp.stack([grad_cols] * lax.axis_size("fsdp")), "fsdp", 0, 0), axis=0
+    )
     pol_hidden = hidden_all[:, unit_count : 2 * unit_count]
     grad_down = grouped_product(pol_hidden, grad_cols_all, groups, members)
     grad_hidden = sent_and_summed(

time: 707 us -> 666 us (0.942)
  waiting for transfers between devices: 293 us -> 219 us
  blocking collectives: 301 us -> 335 us
    all_gather x1 -> x0, waiting for transfers between devices: 74.4 us -> none  [local(): grad_cols_all = lax.all_gather(grad_cols, 'fsdp', axis=0, tiled=True)]
    all_to_all x0 -> x1, blocking collectives: none -> 30.2 us  [local(): lax.all_to_all(jnp.stack([grad_cols] * lax.axis_size('fsdp')), 'fsdp', 0, 0)]
  transfers between devices with their start and end apart: 8 -> 7, of which waited for: 7 -> 6; matrix products, arithmetic and copies ran while one was open for 5% -> 5% of each run, Pallas kernels for 0% -> 0%
where the time goes in v1:
time: 666 us; the launch traced here: 664 us
  blocking collectives  335 us (50%)
  waiting for transfers between devices  219 us (33%)
  local copies, waits for them, and re-layouts  35.3 us (5%)
  starting transfers between devices  29 us (4%)
  other arithmetic  19 us (3%)
  between operations  14.4 us (2%)
  matrix products  13.2 us (2%)
    all_to_all x2, blocking collectives, sent_and_summed(): lax.all_to_all(tiles, axis, split_axis=0, concat_axis=0, tiled=True)  224 us
    all_to_all x1, waiting for transfers between devices, sent_and_summed(): lax.all_to_all(tiles, axis, split_axis=0, concat_axis=0, tiled=True)  102 us
    all_gather x1, waiting for transfers between devices, local(): normed_cols = lax.all_gather(normed_mixed, 'fsdp', axis=0, tiled=True)  72.1 us
    all_to_all x2, blocking collectives, copy_for_each(): return lax.all_to_all(copies, axis, split_axis=0, concat_axis=0, tiled=True)  69 us
    all_to_all x4, waiting for transfers between devices, copy_for_each(): return lax.all_to_all(copies, axis, split_axis=0, concat_axis=0, tiled=True)  44.3 us
    all_to_all x1, blocking collectives, local(): lax.all_to_all(jnp.stack([grad_cols] * lax.axis_size('fsdp')), 'fsdp', 0, 0)  30.2 us
    all_to_all x4, starting transfers between devices, copy_for_each(): return lax.all_to_all(copies, axis, split_axis=0, concat_axis=0, tiled=True)  19.3 us
  transfers between devices with their start and end apart: 7, of which 6 were waited for; matrix products, arithmetic and copies ran while one was open for 5% of the time, Pallas kernels for 0%

profile of v1, /device:TPU:1, one launch (start us, length us, event | category | flops | bytes accessed | tf_op | source)
XLA Modules:
  0.0 664.5 jit_solution(15630877110212280386)
XLA Ops:
  9.0 12.2 %all_to_all.85 = bf16[4,8,512]{2,0,1:T(4,128)(2,1)S(1)} all-to-all(bf16[4,8,512]{2,0,1:T(4,128)(2,1)S(1)} %bitcast.85), channel_id=1, replica_groups=mesh['dp'=8,'fsdp'=32] {'dp'}, dimensions={1} | all-to-all | bytes 65536 | tf_op jit(solution)/shard_map/all_to_all | solution.py:179
  21.8 8.4 %concatenate.16 = bf16[512,1848]{0,1:T(8,128)(2,1)S(1)} concatenate(bf16[512,462]{0,1:T(8,128)(2,1)} %param.15, bf16[512,462]{0,1:T(8,128)(2,1)} %param.16, bf16[512,462]{0,1:T(8,128)(2,1)} %param.18, bf16[512,462]{0,1:T(8,128)(2,1)} %param.19), dimensions={1} | concatenate | bytes 3784704 | tf_op jit(solution)/shard_map/concatenate | solution.py:97
  30.3 72.1 %all-gather.2.cloned.1.call-done = bf16[1024,512]{1,0:T(8,128)(2,1)} async-done(((bf16[32,512]{1,0:T(8,128)(2,1)}), bf16[1024,512]{1,0:T(8,128)(2,1)}) %all-gather.2.cloned.1.call-update) | async-done | bytes 1048592 | tf_op jit(solution)/shard_map/all_gather | solution.py:182
  102.4 3.4 convolution_bitcast_fusion
  106.3 171.0 %all_to_all.86 = f32[8,128,1848]{1,2,0:T(8,128)} all-to-all(f32[8,128,1848]{1,2,0:T(8,128)S(1)} %bitcast.76), channel_id=1, replica_groups=mesh['dp'=8,'fsdp'=32] {'dp'}, dimensions={0} | all-to-all | bytes 15138816 | tf_op jit(solution)/shard_map/all_to_all | solution.py:19
  277.3 3.6 reduce_sum.129
  282.1 47.5 %all_to_all.87 = bf16[8,128,924]{1,2,0:T(8,128)(2,1)S(1)} all-to-all(bf16[8,128,924]{1,2,0:T(8,128)(2,1)S(1)} %broadcast_in_dim.17), channel_id=1, replica_groups=mesh['dp'=8,'fsdp'=32] {'dp'}, dimensions={0} | all-to-all | bytes 3784704 | tf_op jit(solution)/shard_map/all_to_all | solution.py:25
  330.2 4.0 all-to-all-start.5
  335.6 2.1 fusion.28
  339.0 4.6 all-to-all-start.1
  343.6 4.1 pad_maximum_fusion
  347.7 5.3 copy.69
  353.1 5.0 all-to-all-start.4
  359.7 102.3 %all-to-all-done.4 = f32[32,32,1024]{2,1,0:T(8,128)} async-done(((f32[32,32,1024]{2,1,0:T(8,128)}), f32[32,32,1024]{2,1,0:T(8,128)}, u32[]{:S(2)}, u32[]{:S(2)}) %all-to-all-start.4) | async-done | bytes 4194336 | tf_op jit(solution)/shard_map/all_to_all | solution.py:19
  462.0 2.4 reduce_sum.130
  465.6 4.9 all-to-all-start.6
  470.6 4.9 all-to-all-done.6
  475.8 21.5 %all_to_all.88 = f32[32,1,32]{2,1,0:T(1,128)S(1)} all-to-all(f32[32,1,32]{2,1,0:T(1,128)S(1)} %broadcast_in_dim.21), channel_id=1, replica_groups=mesh['dp'=8,'fsdp'=32] {'fsdp'}, dimensions={0} | all-to-all | bytes 8192 | tf_op jit(solution)/shard_map/all_to_all | solution.py:25
  498.3 5.3 all-to-all-start.8
  503.7 4.8 all-to-all-done.8
  508.8 30.2 %all_to_all.89 = bf16[32,32,512]{2,1,0:T(8,128)(2,1)S(1)} all-to-all(bf16[32,32,512]{2,1,0:T(8,128)(2,1)S(1)} %stack.29), channel_id=1, replica_groups=mesh['dp'=8,'fsdp'=32] {'fsdp'}, dimensions={0} | all-to-all | bytes 2097152 | tf_op jit(solution)/shard_map/all_to_all | solution.py:209
  539.7 52.6 %all_to_all.90 = f32[8,128,462]{1,2,0:T(8,128)S(1)} all-to-all(f32[8,128,462]{1,2,0:T(8,128)S(1)} %fusion.5), channel_id=1, replica_groups=mesh['dp'=8,'fsdp'=32] {'dp'}, dimensions={0} | all-to-all | bytes 3784704 | tf_op jit(solution)/shard_map/all_to_all | solution.py:19
  594.4 1.5 broadcast_in_dim.44
  595.9 5.1 all-to-all-start.11
  601.0 2.2 reshape.111
  604.3 1.5 copy.74
  609.4 1.5 convert_reduce_fusion.1
  610.9 34.1 %all-to-all-done.11 = bf16[8,128,924]{1,2,0:T(8,128)(2,1)} async-done(((bf16[8,128,924]{1,2,0:T(8,128)(2,1)}), bf16[8,128,924]{1,2,0:T(8,128)(2,1)}, u32[]{:S(2)}, u32[]{:S(2)}) %all-to-all-start.11) | async-done | bytes 1892384 | tf_op jit(solution)/shard_map/all_to_all | solution.py:25
  645.0 2.8 copy.71
  647.8 2.2 reshape_reshape.6
  650.0 5.0 bitcast_convert_fusion
  656.2 1.5 fusion.32
  (84 shorter events, 20.6 us)
Async XLA Ops:
  7.2 328.4 %copy-start = (bf16[462,512]{1,0:T(8,128)(2,1)S(1)}, bf16[462,512]{1,0:T(8,128)(2,1)}, u32[]{:S(2)}) copy-start(bf16[462,512]{1,0:T(8,128)(2,1)} %param.20) | copy-start | bytes 1419268
  7.2 95.2 %all-gather.2.cloned.1.call-start = ((), (), s32[]{:S(2)}) async-start(), calls=%async_computation.12 | async-start | bytes 1081344 | tf_op jit(solution)/shard_map/all_gather | solution.py:182
  280.9 0.9 copy-start.3
  282.1 47.5 %copy-start.7 = (s32[4]{0:T(128)S(1)}, s32[4]{0:T(128)}, u32[]{:S(2)}) copy-start(s32[4]{0:T(128)} %param.13) | copy-start | bytes 52
  330.2 8.8 %all-to-all-start.5 = ((s32[8,1,4]{2,1,0:T(1,128)}), s32[8,1,4]{2,1,0:T(1,128)S(1)}, u32[]{:S(2)}, u32[]{:S(2)}) async-start(s32[8,1,4]{2,1,0:T(1,128)} %broadcast_in_dim.18), calls=%async_computation.5 | async-start | bytes 8192 | tf_op jit(solution)/shard_map/all_to_all | solution.py:25
  335.6 2.1 copy-start.1
  335.6 2.1 copy-start.5
  339.0 14.1 %all-to-all-start.1 = ((bf16[4,8,512]{2,0,1:T(4,128)(2,1)}), bf16[4,8,512]{2,0,1:T(4,128)(2,1)S(1)}, u32[]{:S(2)}, u32[]{:S(2)}) async-start(bf16[4,8,512]{2,0,1:T(4,128)(2,1)} %bitcast.4), calls=%async_computation.1 | async-start | bytes 65536 | tf_op jit(solution)/shard_map/all_to_all | solution.py:180
  353.1 5.0 copy-start.8
  353.1 108.9 %all-to-all-start.4 = ((f32[32,32,1024]{2,1,0:T(8,128)}), f32[32,32,1024]{2,1,0:T(8,128)}, u32[]{:S(2)}, u32[]{:S(2)}) async-start(f32[32,32,1024]{2,1,0:T(8,128)} %bitcast.77), calls=%async_computation.4 | async-start | bytes 8388608 | tf_op jit(solution)/shard_map/all_to_all | solution.py:19
  359.7 137.7 %copy-start.9 = (f32[1,32]{1,0:T(1,128)S(1)}, f32[1,32]{1,0:T(1,128)}, u32[]{:S(2)}) copy-start(f32[1,32]{1,0:T(1,128)} %param.23) | copy-start | bytes 388
  359.7 137.7 %copy-start.6 = (s32[1,32]{1,0:T(1,128)S(1)}, s32[1,32]{1,0:T(1,128)}, u32[]{:S(2)}) copy-start(s32[1,32]{1,0:T(1,128)} %param.22) | copy-start | bytes 388
  465.6 9.8 %all-to-all-start.6 = ((f32[8,96,2]{1,2,0:T(2,128)}), f32[8,96,2]{1,2,0:T(2,128)S(1)}, u32[]{:S(2)}, u32[]{:S(2)}) async-start(f32[8,96,2]{1,2,0:T(2,128)} %broadcast_in_dim.20), calls=%async_computation.6 | async-start | bytes 16384 | tf_op jit(solution)/shard_map/all_to_all | solution.py:25
  497.6 42.1 %copy-start.10 = (f32[1,32]{1,0:T(1,128)}, f32[1,32]{1,0:T(1,128)S(1)}, u32[]{:S(2)}) copy-start(f32[1,32]{1,0:T(1,128)S(1)} %fusion.25) | copy-start | bytes 388
  498.3 10.2 %all-to-all-start.8 = ((f32[8,1,4]{2,1,0:T(1,128)}), f32[8,1,4]{2,1,0:T(1,128)S(1)}, u32[]{:S(2)}, u32[]{:S(2)}) async-start(f32[8,1,4]{2,1,0:T(1,128)} %broadcast_in_dim.22), calls=%async_computation.8 | async-start | bytes 8192 | tf_op jit(solution)/shard_map/all_to_all | solution.py:25
  595.9 7.2 %copy-start.2 = (bf16[116,8,8,128]{3,1,2,0:T(8,128)(2,1)S(1)}, bf16[116,8,8,128]{3,1,2,0:T(8,128)(2,1)}, u32[]{:S(2)}) copy-start(bf16[116,8,8,128]{3,1,2,0:T(8,128)(2,1)} %copy-done.1) | copy-start | bytes 5701636
  595.9 49.1 %all-to-all-start.11 = ((bf16[8,128,924]{1,2,0:T(8,128)(2,1)}), bf16[8,128,924]{1,2,0:T(8,128)(2,1)}, u32[]{:S(2)}, u32[]{:S(2)}) async-start(bf16[8,128,924]{1,2,0:T(8,128)(2,1)} %broadcast_in_dim.44), calls=%async_computation.11 | async-start | bytes 3801088 | tf_op jit(solution)/shard_map/all_to_all | solution.py:25
  607.0 1.2 copy-start.4
Sparse Core Ops, SparseCore 0:
  22.0 80.3 all-gather.1
